TPU v7x, 128 devices: a whole 4x4x4 slice. The times are simulated.
128 devices in a mesh: ex: 32 (over z, x, y_lo), feat: 4 (over y_hi, core).
Axes of the slice: x: 4, y: 4 (y_hi: 2, y_lo: 2; y = y_hi * 2 + y_lo), z: 4, core: 2. Of those that a mesh axis runs over, the one named last changes fastest.
Arguments:
- train_grads: bfloat16 [12288, 16384], P('ex', 'feat'), may hold values from -6 to 6
- projection: bfloat16 [16384, 4096], P('feat', 'ex'), may hold values from -0.046875 to 0.046875
- test_features: bfloat16 [1024, 4096], P('ex', 'feat'), may hold values from -0.09375 to 0.09375
- example_weights: float32 [12288], P('ex'), may hold values from 0.05 to 1
Outputs:
- scores: float32 [1024, 12288], P('feat', 'ex')
- projected: bfloat16 [12288, 4096], P('ex', 'feat')
All inputs are finite; a program needn't handle non-finite values.
Results may differ from a plain program's by a relative error of at most 0.0031.
Values may be sent and summed in bfloat16 or wider, within the bound.
A program may use at most 192 MiB of HBM per device.

v0:
```python
import jax
import jax.numpy as jnp
from jax import lax
from jax.sharding import Mesh
from jax.sharding import PartitionSpec as P

EX = ("ex_0", "ex_1", "ex_2")


def joined_along(pieces, dim):
    pieces = jnp.moveaxis(pieces, 0, dim)
    dims = pieces.shape
    return pieces.reshape(*dims[:dim], dims[dim] * dims[dim + 1], *dims[dim + 2 :])


def stacked_from(shard, axes, turns):
    pieces = shard[None]
    for k in turns:
        pieces = lax.all_gather(pieces, axes[k], axis=0, tiled=True)
    carried = [lax.axis_size(axes[k]) for k in reversed(turns)]
    pieces = pieces.reshape(*carried, *shard.shape)
    turned = sorted(range(len(turns)), key=lambda place: turns[len(turns) - 1 - place])
    return pieces.transpose(*turned, *range(len(turns), pieces.ndim)).reshape(-1, *shard.shape)


def gather_axes(shard, axes, turns, dim):
    return joined_along(stacked_from(shard, axes, turns), dim)


def in_blocks(shard, dim, length):
    before, after = (shard.shape[:dim], shard.shape[dim + 1 :])
    return jnp.moveaxis(shard.reshape(*before, length, -1, *after), dim, 0)


def summed_on_arrival(shard, axis, dim):
    length = lax.axis_size(axis)
    pieces = lax.all_to_all(in_blocks(shard, dim, length), axis, 0, 0, tiled=True)
    return jnp.sum(pieces, axis=0)


def local(train_grads, projection, test_features, example_weights):
    partial_value = jnp.dot(
        train_grads, gather_axes(projection, EX, (2, 0, 1), 1), preferred_element_type=jnp.float32
    )
    projected = lax.psum_scatter(partial_value, "feat", scatter_dimension=1, tiled=True).astype(
        jnp.bfloat16
    )
    partial_scores = lax.dot_general(
        lax.all_gather(test_features, EX, axis=0, tiled=True),
        projected,
        (((1,), (1,)), ((), ())),
        preferred_element_type=jnp.float32,
    )
    inner = summed_on_arrival(partial_scores, "feat", 0)
    return (inner * example_weights[None, :], projected)


def solution(mesh):
    finer = Mesh(
        mesh.devices.reshape(4, 4, 2, mesh.shape["feat"]), ("ex_0", "ex_1", "ex_2", "feat")
    )
    placed = (P(EX, "feat"), P("feat", EX), P(EX, "feat"), P(EX))
    return jax.shard_map(
        local,
        mesh=finer,
        in_specs=placed,
        out_specs=(P("feat", EX), P(EX, "feat")),
        check_vma=False,
    )
```

profile of v0, /device:TPU:1, one launch (start us, length us, event | category | flops | bytes accessed | tf_op | source)
XLA Modules:
  0.0 740.3 jit_solution(1886742789507018610)
XLA Ops:
  8.0 0.0 all-gather.12.cloned.1.call-start
  8.1 0.7 all-gather.12.cloned.1.call-update
  8.7 0.0 all-gather.6.cloned.1.call-start
  8.8 40.4 %all-gather.12.cloned.1.call-done = bf16[8192,128]{1,0:T(8,128)(2,1)} async-done(((bf16[4096,128]{1,0:T(8,128)(2,1)}), bf16[8192,128]{1,0:T(8,128)(2,1)}) %all-gather.12.cloned.1.call-update) | async-done | bytes 2097168 | tf_op jit(solution)/shard_map/all_gather | solution.py:19
  49.2 0.0 all-gather.6.cloned.1.call-update
  49.2 0.0 all-gather.8.cloned.1.call-start
  49.2 85.9 %all-gather.6.cloned.1.call-done = bf16[8,4096,128]{2,1,0:T(8,128)(2,1)} async-done(((bf16[2,4096,128]{2,1,0:T(8,128)(2,1)}), bf16[8,4096,128]{2,1,0:T(8,128)(2,1)}) %all-gather.6.cloned.1.call-update) | async-done | bytes 8388624 | tf_op jit(solution)/shard_map/all_gather | solution.py:19
  135.1 0.0 all-gather.8.cloned.1.call-update
  135.1 0.0 reduce-scatter.2.cloned.1.call-start
  135.2 296.2 %all-gather.8.cloned.1.call-done = bf16[32,4096,128]{2,1,0:T(8,128)(2,1)} async-done(((bf16[8,4096,128]{2,1,0:T(8,128)(2,1)}), bf16[32,4096,128]{2,1,0:T(8,128)(2,1)}) %all-gather.8.cloned.1.call-update) | async-done | bytes 33554448 | tf_op jit(solution)/shard_map/all_gather | solution.py:19
  431.4 22.9 %copy.9 = bf16[4,4,2,4096,128]{4,3,2,1,0:T(8,128)(2,1)} copy(bf16[4,4,2,4096,128]{4,3,2,0,1:T(8,128)(2,1)} %bitcast.18) | data formatting | bytes 67108864 | tf_op jit(solution)/shard_map/transpose | solution.py:23
  454.3 41.1 %copy.10 = bf16[4096,32,128]{0,2,1:T(8,128)(2,1)} copy(bf16[4096,32,128]{2,0,1:T(8,128)(2,1)} %bitcast.17) | data formatting | bytes 67108864 | tf_op jit(solution)/shard_map/transpose | solution.py:11
  495.4 19.8 %fusion = f32[384,4096]{1,0:T(8,128)} fusion(bf16[384,4096]{1,0:T(8,128)(2,1)S(1)} %copy-done, bf16[4096,4096]{0,1:T(8,128)(2,1)} %bitcast.19), kind=kOutput, calls=%fused_computation.2 | convolution fusion | flops 12884901888 | bytes 42991616 | tf_op jit(solution)/shard_map/dot_general | solution.py:42
  515.3 0.0 all-gather.10.cloned.1.call-start
  515.3 0.5 all-gather.10.cloned.1.call-update
  515.8 66.9 %reduce-scatter.2.cloned.1.call-done = f32[384,1024]{1,0:T(8,128)} async-done(((f32[384,4096]{1,0:T(8,128)}), f32[384,1024]{1,0:T(8,128)}) %reduce-scatter.2.cloned.1.call-update) | async-done | bytes 1572880 | tf_op jit(solution)/shard_map/reduce_scatter | solution.py:45
  582.7 1.5 convert_element_type.3
  584.3 94.7 %all-gather.10.cloned.1.call-done = bf16[1024,1024]{1,0:T(8,128)(2,1)} async-done(((bf16[32,1024]{1,0:T(8,128)(2,1)}), bf16[1024,1024]{1,0:T(8,128)(2,1)}) %all-gather.10.cloned.1.call-update) | async-done | bytes 2097168 | tf_op jit(solution)/shard_map/all_gather | solution.py:49
  679.0 2.6 fusion.1
  681.7 0.1 copy.17
  681.8 47.0 %all_to_all.5 = f32[4,256,384]{1,2,0:T(8,128)} all-to-all(f32[4,256,384]{1,2,0:T(8,128)S(1)} %bitcast.20), channel_id=1, replica_groups=mesh['ex_0'=4,'ex_1'=4,'ex_2'=2,'feat'=4] {'feat'}, dimensions={0} | all-to-all | bytes 3145728 | tf_op jit(solution)/shard_map/all_to_all | solution.py:37
  728.8 2.3 reduce_sum.9
  731.1 1.1 broadcast_multiply_fusion
  732.2 0.9 copy.13
  (9 shorter events, 0.0 us)
Async XLA Ops:
  8.0 487.4 %copy-start = (bf16[384,4096]{1,0:T(8,128)(2,1)S(1)}, bf16[384,4096]{1,0:T(8,128)(2,1)}, u32[]{:S(2)}) copy-start(bf16[384,4096]{1,0:T(8,128)(2,1)} %param.4) | copy-start | bytes 9437188
  8.0 41.1 %all-gather.12.cloned.1.call-start = ((), (), s32[]{:S(2)}) async-start(), calls=%async_computation.6 | async-start | bytes 3145728 | tf_op jit(solution)/shard_map/all_gather | solution.py:19
  8.7 126.4 %all-gather.6.cloned.1.call-start = ((), (), s32[]{:S(2)}) async-start(), calls=%async_computation.2 | async-start | bytes 10485760 | tf_op jit(solution)/shard_map/all_gather | solution.py:19
  49.2 382.2 %all-gather.8.cloned.1.call-start = ((), (), s32[]{:S(2)}) async-start(), calls=%async_computation.3 | async-start | bytes 41943040 | tf_op jit(solution)/shard_map/all_gather | solution.py:19
  135.1 447.6 %reduce-scatter.2.cloned.1.call-start = ((), (), s32[]{:S(2)}) async-start(), calls=%async_computation.4 | async-start | bytes 7864320 | tf_op jit(solution)/shard_map/reduce_scatter | solution.py:45
  515.3 163.8 %all-gather.10.cloned.1.call-start = ((), (), s32[]{:S(2)}) async-start(), calls=%async_computation.5 | async-start | bytes 2162688 | tf_op jit(solution)/shard_map/all_gather | solution.py:49
  584.3 97.4 %copy-start.2 = (bf16[384,1024]{1,0:T(8,128)(2,1)}, bf16[384,1024]{1,0:T(8,128)(2,1)S(1)}, u32[]{:S(2)}) copy-start(bf16[384,1024]{1,0:T(8,128)(2,1)S(1)} %convert_element_type.3) | copy-start | bytes 2359300
  681.8 49.3 %copy-start.3 = (f32[384]{0:T(512)S(1)}, f32[384]{0:T(512)}, u32[]{:S(2)}) copy-start(f32[384]{0:T(512)} %param.7) | copy-start | bytes 4612
  681.8 51.3 %copy-start.1 = (bf16[384,4096]{1,0:T(8,128)(2,1)S(1)}, bf16[384,4096]{1,0:T(8,128)(2,1)}, u32[]{:S(2)}) copy-start(bf16[384,4096]{1,0:T(8,128)(2,1)} %param.4) | copy-start | bytes 9437188
Sparse Core Ops, SparseCore 0:
  10.5 38.6 all-gather.11
  50.8 84.2 all-gather.5
  136.8 294.5 all-gather.7
  515.4 67.3 reduce-scatter.1
Sparse Core Ops, SparseCore 1:
  517.4 161.6 all-gather.9
where the time goes:
time: 742 us; the launch traced here: 740 us
  waiting for transfers between devices  585 us (79%)
  local copies, waits for them, and re-layouts  65.1 us (9%)
  blocking collectives  47 us (6%)
  matrix products  22.4 us (3%)
  between operations  15.3 us (2%)
    all_gather x3, waiting for transfers between devices, stacked_from(): pieces = lax.all_gather(pieces, axes[k], axis=0, tiled=True)  422 us
    all_gather x1, waiting for transfers between devices, local(): lax.all_gather(test_features, EX, axis=0, tiled=True)  94.7 us
    reduce_scatter x1, waiting for transfers between devices, local(): lax.psum_scatter(partial_value, 'feat', scatter_dimension=1, tiled=True)  66.9 us
    all_to_all x1, blocking collectives, summed_on_arrival(): lax.all_to_all(in_blocks(shard, dim, length), axis, 0, 0, tiled=True)  47 us
    transpose x1, local copies, waits for them, and re-layouts, joined_along(): pieces = jnp.moveaxis(pieces, 0, dim)  41.1 us
    transpose x1, local copies, waits for them, and re-layouts, stacked_from(): pieces.transpose(*turned, *range(len(turns), pieces.ndim))  22.9 us
    dot_general x1, matrix products, local(): jnp.dot(train_grads, gather_axes(projection, EX, (2, 0, 1), 1), preferred...  19.8 us
  transfers between devices with their start and end apart: 5, of which 5 were waited for; matrix products, arithmetic and copies ran while one was open for 0% of the time, Pallas kernels for 0%

commit v1 on v0

--- a/solution.py
+++ b/solution.py
@@ -16,7 +16,9 @@
 def stacked_from(shard, axes, turns):
     pieces = shard[None]
     for k in turns:
-        pieces = lax.all_gather(pieces, axes[k], axis=0, tiled=True)
+        pieces = jnp.concatenate(
+            lax.all_to_all(jnp.stack([pieces] * lax.axis_size(axes[k])), axes[k], 0, 0), axis=0
+        )
     carried = [lax.axis_size(axes[k]) for k in reversed(turns)]
     pieces = pieces.reshape(*carried, *shard.shape)
     turned = sorted(range(len(turns)), key=lambda place: turns[len(turns) - 1 - place])

time: 742 us -> 846 us (1.14)
  blocking collectives: 47 us -> 503 us
  waiting for transfers between devices: 585 us -> 179 us
  starting transfers between devices: 0.2 us -> 27.6 us
  local copies, waits for them, and re-layouts: 65.1 us -> 84.2 us
    all_to_all x1 -> x3, blocking collectives: 47 us -> 503 us  [stacked_from(): lax.all_to_all(jnp.stack([pieces] * lax.axis_size(axes[k])), axes[k], 0, 0)]
    all_gather x3 -> x0, waiting for transfers between devices: 422 us -> none  [stacked_from(): pieces = lax.all_gather(pieces, axes[k], axis=0, tiled=True)]
    all_to_all x0 -> x1, starting transfers between devices: none -> 27.5 us  [summed_on_arrival(): lax.all_to_all(in_blocks(shard, dim, length), axis, 0, 0, tiled=True)]
    all_to_all x0 -> x1, waiting for transfers between devices: none -> 18.4 us  [summed_on_arrival(): lax.all_to_all(in_blocks(shard, dim, length), axis, 0, 0, tiled=True)]
    another operation x0 -> x2, local copies, waits for them, and re-layouts: none -> 15.3 us  [stacked_from(): jnp.stack([pieces] * lax.axis_size(axes[k]))]
  transfers between devices with their start and end apart: 5 -> 3, of which waited for: 5 -> 3; matrix products, arithmetic and copies ran while one was open for 0% -> 1% of each run, Pallas kernels for 0% -> 0%
where the time goes in v1:
time: 846 us; the launch traced here: 844 us
  blocking collectives  503 us (59%)
  waiting for transfers between devices  179 us (21%)
  local copies, waits for them, and re-layouts  84.2 us (10%)
  starting transfers between devices  27.6 us (3%)
  matrix products  26.5 us (3%)
  between operations  15.5 us (2%)
    all_to_all x3, blocking collectives, stacked_from(): lax.all_to_all(jnp.stack([pieces] * lax.axis_size(axes[k])), axes[k], 0, 0)  503 us
    all_gather x1, waiting for transfers between devices, local(): lax.all_gather(test_features, EX, axis=0, tiled=True)  93.4 us
    reduce_scatter x1, waiting for transfers between devices, local(): lax.psum_scatter(partial_value, 'feat', scatter_dimension=1, tiled=True)  67.2 us
    transpose x1, local copies, waits for them, and re-layouts, joined_along(): pieces = jnp.moveaxis(pieces, 0, dim)  41.5 us
    all_to_all x1, starting transfers between devices, summed_on_arrival(): lax.all_to_all(in_blocks(shard, dim, length), axis, 0, 0, tiled=True)  27.5 us
    dot_general x1, matrix products, local(): jnp.dot(train_grads, gather_axes(projection, EX, (2, 0, 1), 1), preferred...  23.6 us
    transpose x1, local copies, waits for them, and re-layouts, stacked_from(): pieces.transpose(*turned, *range(len(turns), pieces.ndim))  22.8 us
    all_to_all x1, waiting for transfers between devices, summed_on_arrival(): lax.all_to_all(in_blocks(shard, dim, length), axis, 0, 0, tiled=True)  18.4 us
  transfers between devices with their start and end apart: 3, of which 3 were waited for; matrix products, arithmetic and copies ran while one was open for 1% of the time, Pallas kernels for 0%

profile of v1, /device:TPU:1, one launch (start us, length us, event | category | flops | bytes accessed | tf_op | source)
XLA Modules:
  0.0 843.9 jit_solution(3687870152594547294)
XLA Ops:
  8.0 0.0 reduce-scatter.2.cloned.1.call-start
  8.1 1.9 pad_maximum_fusion
  9.9 27.2 %all_to_all.20 = bf16[2,1,4096,128]{3,2,1,0:T(8,128)(2,1)S(1)} all-to-all(bf16[2,1,4096,128]{3,2,1,0:T(8,128)(2,1)S(1)} %pad_maximum_fusion), channel_id=1, replica_groups=mesh['ex_0'=4,'ex_1'=4,'ex_2'=2,'feat'=4] {'ex_2'}, dimensions={0} | all-to-all | bytes 4194304 | tf_op jit(solution)/shard_map/all_to_all | solution.py:20
  37.1 4.3 stack.10
  41.4 97.3 %all_to_all.21 = bf16[4,2,4096,128]{3,2,1,0:T(8,128)(2,1)S(1)} all-to-all(bf16[4,2,4096,128]{3,2,1,0:T(8,128)(2,1)} %stack.10), channel_id=1, replica_groups=mesh['ex_0'=4,'ex_1'=4,'ex_2'=2,'feat'=4] {'ex_0'}, dimensions={0} | all-to-all | bytes 16777216 | tf_op jit(solution)/shard_map/all_to_all | solution.py:20
  138.7 11.1 %stack.11 = bf16[4,8,4096,128]{3,2,1,0:T(8,128)(2,1)} broadcast(bf16[8,4096,128]{2,1,0:T(8,128)(2,1)S(1)} %bitcast.23), dimensions={1,2,3} | broadcast | bytes 41943040 | tf_op jit(solution)/shard_map/stack | solution.py:20
  149.8 378.6 %all_to_all.22 = bf16[4,8,4096,128]{3,2,1,0:T(8,128)(2,1)} all-to-all(bf16[4,8,4096,128]{3,2,1,0:T(8,128)(2,1)} %stack.11), channel_id=1, replica_groups=mesh['ex_0'=4,'ex_1'=4,'ex_2'=2,'feat'=4] {'ex_1'}, dimensions={0} | all-to-all | bytes 67108864 | tf_op jit(solution)/shard_map/all_to_all | solution.py:20
  528.4 22.8 %copy.12 = bf16[4,4,2,4096,128]{4,3,2,1,0:T(8,128)(2,1)} copy(bf16[4,4,2,4096,128]{4,3,2,0,1:T(8,128)(2,1)} %bitcast.21) | data formatting | bytes 67108864 | tf_op jit(solution)/shard_map/transpose | solution.py:25
  551.2 41.5 %copy.13 = bf16[4096,32,128]{0,2,1:T(8,128)(2,1)} copy(bf16[4096,32,128]{2,0,1:T(8,128)(2,1)} %bitcast.22) | data formatting | bytes 67108864 | tf_op jit(solution)/shard_map/transpose | solution.py:11
  592.7 23.6 %convolution_bitcast_fusion = f32[384,4096]{0,1:T(8,128)} fusion(bf16[4096,4096]{0,1:T(8,128)(2,1)} %bitcast.24, bf16[384,4096]{1,0:T(8,128)(2,1)S(1)} %copy-done), kind=kOutput, calls=%fused_computation | convolution fusion | flops 12884901888 | bytes 42991616 | tf_op jit(solution)/shard_map/dot_general | solution.py:44
  616.4 0.0 reduce-scatter.2.cloned.1.call-update
  616.4 0.0 all-gather.2.cloned.1.call-start
  616.4 0.5 all-gather.2.cloned.1.call-update
  617.0 67.2 %reduce-scatter.2.cloned.1.call-done = f32[384,1024]{0,1:T(8,128)} async-done(((f32[384,4096]{0,1:T(8,128)}), f32[384,1024]{0,1:T(8,128)}) %reduce-scatter.2.cloned.1.call-update) | async-done | bytes 1572880 | tf_op jit(solution)/shard_map/reduce_scatter | solution.py:47
  684.1 2.4 convert_element_type.3
  686.5 93.4 %all-gather.2.cloned.1.call-done = bf16[1024,1024]{1,0:T(8,128)(2,1)} async-done(((bf16[32,1024]{1,0:T(8,128)(2,1)}), bf16[1024,1024]{1,0:T(8,128)(2,1)}) %all-gather.2.cloned.1.call-update) | async-done | bytes 2097168 | tf_op jit(solution)/shard_map/all_gather | solution.py:51
  779.8 2.9 fusion
  782.7 1.3 copy.21
  784.0 27.5 %all-to-all-start.3 = ((f32[4,256,384]{1,2,0:T(8,128)}), f32[4,256,384]{1,2,0:T(8,128)}, u32[]{:S(2)}, u32[]{:S(2)}) async-start(f32[4,256,384]{1,2,0:T(8,128)} %bitcast.26), calls=%async_computation.4 | async-start | bytes 3145728 | tf_op jit(solution)/shard_map/all_to_all | solution.py:39
  811.5 2.3 copy.17
  813.8 18.4 %all-to-all-done.3 = f32[4,256,384]{1,2,0:T(8,128)} async-done(((f32[4,256,384]{1,2,0:T(8,128)}), f32[4,256,384]{1,2,0:T(8,128)}, u32[]{:S(2)}, u32[]{:S(2)}) %all-to-all-start.3) | async-done | bytes 1572896 | tf_op jit(solution)/shard_map/all_to_all | solution.py:39
  832.2 2.3 reduce_sum.9
  834.5 1.1 broadcast_multiply_fusion
  835.6 0.9 copy.16
  (4 shorter events, 0.0 us)
Async XLA Ops:
  8.0 584.7 %copy-start = (bf16[384,4096]{1,0:T(8,128)(2,1)S(1)}, bf16[384,4096]{1,0:T(8,128)(2,1)}, u32[]{:S(2)}) copy-start(bf16[384,4096]{1,0:T(8,128)(2,1)} %param.4) | copy-start | bytes 9437188
  8.0 676.1 %reduce-scatter.2.cloned.1.call-start = ((), (), s32[]{:S(2)}) async-start(), calls=%async_computation.5 | async-start | bytes 7864320 | tf_op jit(solution)/shard_map/reduce_scatter | solution.py:47
  616.4 163.5 %all-gather.2.cloned.1.call-start = ((), (), s32[]{:S(2)}) async-start(), calls=%async_computation.6 | async-start | bytes 2162688 | tf_op jit(solution)/shard_map/all_gather | solution.py:51
  784.0 50.5 %copy-start.1 = (f32[384]{0:T(512)S(1)}, f32[384]{0:T(512)}, u32[]{:S(2)}) copy-start(f32[384]{0:T(512)} %param.7) | copy-start | bytes 4612
  784.0 48.2 %all-to-all-start.3 = ((f32[4,256,384]{1,2,0:T(8,128)}), f32[4,256,384]{1,2,0:T(8,128)}, u32[]{:S(2)}, u32[]{:S(2)}) async-start(f32[4,256,384]{1,2,0:T(8,128)} %bitcast.26), calls=%async_computation.4 | async-start | bytes 3145728 | tf_op jit(solution)/shard_map/all_to_all | solution.py:39
Sparse Core Ops, SparseCore 0:
  616.5 67.5 reduce-scatter.1
Sparse Core Ops, SparseCore 1:
  618.5 161.3 all-gather.1
